TPU v7x, 32 devices: a whole 2x2x4 slice. The times are simulated.
32 devices in a mesh: grp: 8 (over z, x), node: 4 (over y, core).
Axes of the slice: x: 2, y: 2, z: 4, core: 2. Of those that a mesh axis runs over, the one named last changes fastest.
Arguments:
- initial: float32 [6, 32, 32768], P(None, None, ('grp', 'node')), may hold values from -0.5 to 16, as said below
- afferent_noise_level: float32 [32, 32768], P(None, ('grp', 'node')), may hold values from 0.12 to 0.32
- history: bfloat16 [64, 32, 32768], P(None, None, ('grp', 'node')), may hold values from 0 to 1
- weights: bfloat16 [32, 24, 128, 1024], P(('grp', 'node')), may hold values from -0.109375 to 0.109375
- lead_field: bfloat16 [128, 32768], P(None, ('grp', 'node')), may hold values from -0.00390625 to 0.00390625
- src_group: int32 [32, 24], replicated, may hold values from 0 to 7, as said below
- src_sub: int32 [32, 24], replicated, may hold values from 0 to 7
- delays: int32 [32, 24], replicated, may hold values from 6 to 63
- counts: int32 [32], replicated, may hold values from 16 to 24, as said below
Outputs:
- final_state: float32 [6, 32, 32768], P(None, None, ('grp', 'node'))
- sensors: float32 [6, 128, 32], replicated
Inputs may be any that keep to these rules, and one draw needn't show every extreme that they name: `initial`: rows 0 to 2 are potentials and rows 3 to 5 their rates; row 0 lies within 0 and 0.4, row 1 within 4 and 16, row 2 within 0 and 8, rows 3 to 5 within -0.5 and 0.5. `src_group`: among the tiles k < counts[b] of a block b no owner group appears more than 3 times, and some block reaches 3. Tiles k >= counts[b] of block b are ignored; in every draw some block has 24 live tiles.
All inputs are finite; a program needn't handle non-finite values.
Results may differ from a plain program's by a relative error of at most 0.0003.
The roundings to bfloat16 on the way count: a program that leaves them out, or rounds other values in their place, can miss the bound.
Values may be sent and summed in bfloat16 or wider, within the bound.
A program may use at most 128 MiB of HBM per device.

v0:
```python
import functools

import jax
import jax.numpy as jnp
from jax import lax
from jax.experimental import pallas as pl
from jax.experimental.pallas import tpu as pltpu
from jax.sharding import PartitionSpec as P

DMIN = 6
STEPS = 6
VMEM_BYTES = 67043328
TIME_GROUPS = ((0, 1), (2, 3), (4, 5), (6,))

exciting_amplitude = 3.25
suppressive_amplitude = 22.0
exciting_inverse_lag = 0.1
suppressive_inverse_lag = 0.05
link_factor = 135.0
maximal_spike_frequency = 0.005
thresh = 6.0
fire_slope = 0.56
global_scaling_factor = 0.5
dt_step = 0.5

MESH = pl.DeviceIdType.MESH


def sigmoid_spike_density(level):
    return 1.0 / (1.0 + jnp.exp(fire_slope * (thresh - level)))


def derivative(y, noise, coupled):
    curvature = (
        exciting_amplitude
        * exciting_inverse_lag
        * maximal_spike_frequency
        * sigmoid_spike_density(y[1] - y[2])
        - 2.0 * exciting_inverse_lag * y[3]
        - exciting_inverse_lag * exciting_inverse_lag * y[0]
    )
    interneuron = (
        exciting_amplitude
        * exciting_inverse_lag
        * (
            noise
            + 0.8
            * link_factor
            * maximal_spike_frequency
            * sigmoid_spike_density(link_factor * y[0])
            + global_scaling_factor * coupled
        )
        - 2.0 * exciting_inverse_lag * y[4]
        - exciting_inverse_lag * exciting_inverse_lag * y[1]
    )
    suppressive = (
        suppressive_amplitude
        * suppressive_inverse_lag
        * 0.25
        * link_factor
        * maximal_spike_frequency
        * sigmoid_spike_density(0.25 * link_factor * y[0])
        - 2.0 * suppressive_inverse_lag * y[5]
        - suppressive_inverse_lag * suppressive_inverse_lag * y[2]
    )
    return [y[3], y[4], y[5], curvature, interneuron, suppressive]


def advance(y, noise, coupled_now, coupled_next):
    first = derivative(y, noise, coupled_now)
    moved = [a + dt_step * b for a, b in zip(y, first)]
    second = derivative(moved, noise, coupled_next)
    return [a + 0.5 * dt_step * (b + c) for a, b, c in zip(y, first, second)]


def pack_kernel(
    owners,
    columns,
    slots,
    src_group,
    src_sub,
    delays,
    counts,
    initial_hbm,
    history_hbm,
    own_place,
    *rest,
):
    groups = len(TIME_GROUPS)
    packed = rest[:groups]
    sel_sub, sel_delay, fired, fields, hist, local_sem = rest[groups:]
    me = lax.axis_index("grp")
    column = lax.axis_index("node")
    cycle_len, replicas, block_len = hist.shape
    tiles = src_group.shape[0]
    piece_len = packed[0].shape[3]

    load_fields = pltpu.make_async_copy(initial_hbm.at[pl.ds(1, 2)], fields, local_sem.at[0])
    load_history = pltpu.make_async_copy(history_hbm, hist, local_sem.at[1])
    load_fields.start()
    load_history.start()

    def choose(dest, carry):
        block = dest * columns + column
        live = counts[block]
        rank = jnp.int32(0)
        subs = [jnp.int32(0)] * slots
        waits = [jnp.int32(DMIN)] * slots
        for k in range(tiles):
            hit = jnp.logical_and(src_group[k, block] == me, k < live)
            sub, wait = src_sub[k, block], delays[k, block]
            for r in range(slots):
                take = jnp.logical_and(hit, rank == r)
                subs[r] = jnp.where(take, sub, subs[r])
                waits[r] = jnp.where(take, wait, waits[r])
            rank = rank + jnp.where(hit, 1, 0)
        for r in range(slots):
            sel_sub[dest * slots + r] = subs[r]
            sel_delay[dest * slots + r] = waits[r]
        return carry

    lax.fori_loop(0, owners, choose, 0)

    my_block = me * columns + column
    my_live = counts[my_block]
    my_groups = [src_group[k, my_block] for k in range(tiles)]
    for k in range(tiles):
        rank = jnp.int32(0)
        for earlier in range(k):
            rank = rank + jnp.where(my_groups[earlier] == my_groups[k], 1, 0)
        place = my_groups[k] * slots + jnp.minimum(rank, slots - 1)
        own_place[k] = jnp.where(k < my_live, place, owners * slots)

    load_fields.wait()

    def first_fire(tile, carry):
        cols = pl.ds(pl.multiple_of(tile * piece_len, piece_len), piece_len)
        fire = sigmoid_spike_density(fields[0, :, cols] - fields[1, :, cols])
        fired[:, cols] = fire.astype(jnp.bfloat16)
        return carry

    lax.fori_loop(0, block_len // piece_len, first_fire, 0)

    load_history.wait()

    def pack(place, carry):
        start = cycle_len - sel_delay[place]
        cols = pl.ds(pl.multiple_of(sel_sub[place] * piece_len, piece_len), piece_len)
        for times, parcel in zip(TIME_GROUPS, packed):
            for j, t in enumerate(times):
                if t < DMIN:
                    parcel[place, j] = hist[start + t, :, cols]
                else:
                    past = hist[jnp.minimum(start + t, cycle_len - 1), :, cols]
                    parcel[place, j] = jnp.where(start + t < cycle_len, past, fired[:, cols])
        return carry

    lax.fori_loop(0, owners * slots, pack, 0)


def kernel(
    owners,
    columns,
    slots,
    own_place,
    initial_hbm,
    noise_hbm,
    weights_hbm,
    lead_hbm,
    *rest,
):
    group_count = len(TIME_GROUPS)
    packed = rest[:group_count]
    landed = rest[-group_count:]
    staged = rest[-2 * group_count : -group_count]
    (
        final_hbm,
        sensors_out,
        state,
        noise,
        weights,
        lead,
        lhs,
        coupled,
        potential,
        partial,
        scatter_in,
        node_in,
        gathered,
        local_sem,
        keep_sem,
        stage_sem,
        send_sem,
        recv_sem,
        scatter_send,
        scatter_recv,
        node_send,
        node_recv,
        gather_send,
        gather_recv,
    ) = rest[group_count : -2 * group_count]
    me = lax.axis_index("grp")
    column = lax.axis_index("node")
    mine = pl.ds(me * slots, slots)
    stage = [
        pltpu.make_async_copy(packed[g], staged[g], stage_sem.at[g]) for g in range(group_count)
    ]
    for copy in stage:
        copy.start()
    replicas, block_len = noise.shape
    tiles = own_place.shape[0]
    piece_len = weights.shape[0] // tiles
    offsets = sorted(range(1, owners), key=lambda o: abs(2 * o - owners))

    barrier = pltpu.get_barrier_semaphore()
    for o in offsets:
        pl.semaphore_signal(
            barrier, inc=1, device_id={"grp": lax.rem(me + o, owners)}, device_id_type=MESH
        )
    for o in range(1, columns):
        pl.semaphore_signal(
            barrier, inc=1, device_id={"node": lax.rem(column + o, columns)}, device_id_type=MESH
        )

    spare = owners * slots
    for g in range(group_count):
        landed[g][spare] = jnp.zeros(landed[g].shape[1:], jnp.bfloat16)

    for copy in stage:
        copy.wait()
    keep = [
        pltpu.make_async_copy(packed[g].at[mine], landed[g].at[mine], keep_sem.at[g])
        for g in range(group_count)
    ]
    loads = [
        pltpu.make_async_copy(weights_hbm, weights, local_sem.at[0]),
        pltpu.make_async_copy(initial_hbm, state, local_sem.at[1]),
        pltpu.make_async_copy(noise_hbm, noise, local_sem.at[2]),
        pltpu.make_async_copy(lead_hbm, lead, local_sem.at[3]),
    ]
    for copy in keep + loads:
        copy.start()
    pl.semaphore_wait(barrier, owners + columns - 2)

    def parcel_copy(g, o):
        dest = lax.rem(me + o, owners)
        return pltpu.make_async_remote_copy(
            src_ref=staged[g].at[pl.ds(dest * slots, slots)],
            dst_ref=landed[g].at[mine],
            send_sem=send_sem.at[g, o],
            recv_sem=recv_sem.at[g, o],
            device_id={"grp": dest},
            device_id_type=MESH,
        )

    for g in range(group_count):
        for o in offsets:
            parcel_copy(g, o).start()

    for copy in keep + loads:
        copy.wait()

    dot_cols = min(256, block_len)
    rows_per = replicas
    chunk = partial.shape[1]

    for g, times in enumerate(TIME_GROUPS):
        for o in offsets:
            parcel_copy(g, o).wait_recv()
        rows = len(times) * rows_per
        base = times[0] * rows_per

        for k in range(tiles):
            piece = landed[g][own_place[k]]
            lhs[:rows, k * piece_len : (k + 1) * piece_len] = piece.reshape(rows, piece_len)

        def multiply(tile, carry):
            cols = pl.ds(pl.multiple_of(tile * dot_cols, dot_cols), dot_cols)
            coupled[base : base + rows, cols] = jnp.dot(
                lhs[:rows, :], weights[:, cols], preferred_element_type=jnp.float32
            )
            return carry

        lax.fori_loop(0, block_len // dot_cols, multiply, 0)

        steps = [t - 1 for t in times if t > 0]

        def move(tile, carry):
            cols = pl.ds(pl.multiple_of(tile * piece_len, piece_len), piece_len)
            y = [state[i, :, cols] for i in range(6)]
            drive = noise[:, cols]
            now = coupled[steps[0] * rows_per : (steps[0] + 1) * rows_per, cols]
            for i, s in enumerate(steps):
                later = coupled[(s + 1) * rows_per : (s + 2) * rows_per, cols]
                y = advance(y, drive, now, later)
                now = later
                potential[i * rows_per : (i + 1) * rows_per, cols] = (y[1] - y[2]).astype(
                    jnp.bfloat16
                )
            for i in range(6):
                state[i, :, cols] = y[i]
            return carry

        lax.fori_loop(0, block_len // piece_len, move, 0)

        if g == group_count - 1:
            save_state = pltpu.make_async_copy(state, final_hbm, local_sem.at[4])
            save_state.start()

        signal = lax.dot_general(
            potential[: len(steps) * rows_per, :],
            lead[...],
            (((1,), (1,)), ((), ())),
            preferred_element_type=jnp.float32,
        )
        row = steps[0] * rows_per
        stop = row + len(steps) * rows_per
        first_row = row
        while row < stop:
            part, inside = divmod(row, chunk)
            many = min(chunk - inside, stop - row)
            partial[part, inside : inside + many, :] = signal[
                row - first_row : row - first_row + many, :
            ]
            row += many

    def scatter_copy(o):
        dest = lax.rem(me + o, owners)
        return pltpu.make_async_remote_copy(
            src_ref=partial.at[dest],
            dst_ref=scatter_in.at[o],
            send_sem=scatter_send.at[o],
            recv_sem=scatter_recv.at[o],
            device_id={"grp": dest},
            device_id_type=MESH,
        )

    for o in offsets:
        scatter_copy(o).start()
    for g in range(group_count):
        for o in offsets:
            parcel_copy(g, o).wait_send()
    total = partial[me]
    for o in reversed(offsets):
        scatter_copy(o).wait_recv()
        total = total + scatter_in[o]
    node_in[column] = total

    def node_copy(o):
        return pltpu.make_async_remote_copy(
            src_ref=node_in.at[column],
            dst_ref=node_in.at[column],
            send_sem=node_send.at[o],
            recv_sem=node_recv.at[o],
            device_id={"node": lax.rem(column + o, columns)},
            device_id_type=MESH,
        )

    for o in range(1, columns):
        node_copy(o).start()
    for o in range(1, columns):
        node_copy(o).wait_recv()
    total = node_in[0]
    for c in range(1, columns):
        total = total + node_in[c]
    gathered[me] = total

    def gather_copy(o):
        return pltpu.make_async_remote_copy(
            src_ref=gathered.at[me],
            dst_ref=gathered.at[me],
            send_sem=gather_send.at[o],
            recv_sem=gather_recv.at[o],
            device_id={"grp": lax.rem(me + o, owners)},
            device_id_type=MESH,
        )

    for o in offsets:
        gather_copy(o).start()
    for o in offsets:
        scatter_copy(o).wait_send()
    for o in range(1, columns):
        node_copy(o).wait_send()
    for o in offsets:
        gather_copy(o).wait_recv()
    sensors_out[...] = gathered[...]
    for o in offsets:
        gather_copy(o).wait_send()
    save_state.wait()


def body(
    owners,
    columns,
    initial,
    afferent_noise_level,
    history,
    weights,
    lead_field,
    src_group,
    src_sub,
    delays,
    counts,
):
    cycle_len, replicas, block_len = history.shape
    tiles = src_group.shape[1]
    piece_len = weights.shape[2]
    sensors = lead_field.shape[0]
    slots = (tiles + owners - 1) // owners
    chunk = (STEPS * replicas + owners - 1) // owners
    groups = len(TIME_GROUPS)
    most = max(len(times) for times in TIME_GROUPS) * replicas
    smem = pl.BlockSpec(memory_space=pltpu.SMEM)
    vmem = pl.BlockSpec(memory_space=pltpu.VMEM)
    anywhere = pl.BlockSpec(memory_space=pl.ANY)
    own_place, *packed = pl.pallas_call(
        functools.partial(pack_kernel, owners, columns, slots),
        out_shape=[jax.ShapeDtypeStruct((tiles,), jnp.int32)]
        + [
            jax.ShapeDtypeStruct(
                (owners * slots, len(times), replicas, piece_len), jnp.bfloat16
            )
            for times in TIME_GROUPS
        ],
        in_specs=[smem] * 4 + [anywhere] * 2,
        out_specs=[smem] + [vmem] * groups,
        scratch_shapes=[
            pltpu.SMEM((owners * slots,), jnp.int32),
            pltpu.SMEM((owners * slots,), jnp.int32),
            pltpu.VMEM((replicas, block_len), jnp.bfloat16),
            pltpu.VMEM((2, replicas, block_len), jnp.float32),
            pltpu.VMEM(history.shape, jnp.bfloat16),
            pltpu.SemaphoreType.DMA((2,)),
        ],
        compiler_params=pltpu.CompilerParams(vmem_limit_bytes=VMEM_BYTES),
        cost_estimate=pl.CostEstimate(flops=0, bytes_accessed=8 * 1024 * 1024, transcendentals=0),
    )(src_group.T, src_sub.T, delays.T, counts, initial, history)
    final, signal = pl.pallas_call(
        functools.partial(kernel, owners, columns, slots),
        out_shape=(
            jax.ShapeDtypeStruct(initial.shape, jnp.float32),
            jax.ShapeDtypeStruct((owners, chunk, sensors), jnp.float32),
        ),
        in_specs=[smem] + [anywhere] * (4 + groups),
        out_specs=(anywhere, vmem),
        scratch_shapes=[
            pltpu.VMEM(initial.shape, jnp.float32),
            pltpu.VMEM((replicas, block_len), jnp.float32),
            pltpu.VMEM((tiles * piece_len, block_len), jnp.bfloat16),
            pltpu.VMEM(lead_field.shape, jnp.bfloat16),
            pltpu.VMEM((most, tiles * piece_len), jnp.bfloat16),
            pltpu.VMEM(((STEPS + 1) * replicas, block_len), jnp.float32),
            pltpu.VMEM((most, block_len), jnp.bfloat16),
            pltpu.VMEM((owners, chunk, sensors), jnp.float32),
            pltpu.VMEM((owners, chunk, sensors), jnp.float32),
            pltpu.VMEM((columns, chunk, sensors), jnp.float32),
            pltpu.VMEM((owners, chunk, sensors), jnp.float32),
            pltpu.SemaphoreType.DMA((5,)),
            pltpu.SemaphoreType.DMA((groups,)),
            pltpu.SemaphoreType.DMA((groups,)),
            pltpu.SemaphoreType.DMA((groups, owners)),
            pltpu.SemaphoreType.DMA((groups, owners)),
            pltpu.SemaphoreType.DMA((owners,)),
            pltpu.SemaphoreType.DMA((owners,)),
            pltpu.SemaphoreType.DMA((columns,)),
            pltpu.SemaphoreType.DMA((columns,)),
            pltpu.SemaphoreType.DMA((owners,)),
            pltpu.SemaphoreType.DMA((owners,)),
        ]
        + [
            pltpu.VMEM((owners * slots, len(times), replicas, piece_len), jnp.bfloat16)
            for times in TIME_GROUPS
        ]
        + [
            pltpu.VMEM((owners * slots + 1, len(times), replicas, piece_len), jnp.bfloat16)
            for times in TIME_GROUPS
        ],
        compiler_params=pltpu.CompilerParams(
            collective_id=0, has_side_effects=True, vmem_limit_bytes=VMEM_BYTES
        ),
    )(
        own_place,
        initial,
        afferent_noise_level,
        weights.reshape(tiles * piece_len, block_len),
        lead_field,
        *packed,
    )
    signal = signal.reshape(owners * chunk, sensors)[: STEPS * replicas]
    signal = signal.reshape(STEPS, replicas, sensors)
    return final, jnp.transpose(signal, (0, 2, 1))


def solution(mesh):
    return jax.shard_map(
        functools.partial(body, mesh.shape["grp"], mesh.shape["node"]),
        mesh=mesh,
        in_specs=(
            P(None, None, ("grp", "node")),
            P(None, ("grp", "node")),
            P(None, None, ("grp", "node")),
            P(("grp", "node"), None, None, None),
            P(None, ("grp", "node")),
            P(),
            P(),
            P(),
            P(),
        ),
        out_specs=(P(None, None, ("grp", "node")), P()),
        check_vma=False,
    )
```

profile of v0, /device:TPU:0, one launch (start us, length us, event | category | flops | bytes accessed | tf_op | source)
XLA Modules:
  0.0 64.0 jit_solution(17143897013708407038)
XLA Ops:
  0.6 5.2 %shard_map.104 = (s32[24]{0:T(128)}, bf16[24,2,32,128]{3,2,1,0:T(8,128)(2,1)}, bf16[24,2,32,128]{3,2,1,0:T(8,128)(2,1)}, bf16[24,2,32,128]{3,2,1,0:T(8,128)(2,1)}, bf16[24,1,32,128]{3,2,1,0:T(8,128)(2,1)}) custom-call(s32[24,32]{1,0:T(8,128)} %bitcast.9, s32[24,32]{1,0:T(8,128)} %bitcast.10, s32[24,32]{1,0:T(8,128)} %bitcast.11, s32[32]{0:T(128)} %counts.1, ...), custom_call_target="tpu_custom_call" | custom-call | bytes 8388608 | tf_op jit(solution)/shard_map/pallas_call | solution.py:416
  5.9 54.5 %shard_map.105 = (f32[6,32,1024]{2,1,0:T(8,128)}, f32[8,24,128]{2,1,0:T(8,128)}) custom-call(s32[24]{0:T(128)} %get-tuple-element.9.own_place, f32[6,32,1024]{2,1,0:T(8,128)} %initial_hbm.3, f32[32,1024]{1,0:T(8,128)} %noise_hbm.1, bf16[3072,1024]{1,0:T(8,128)(2,1)} %bitcast.7, bf16[128,1024]{1,0:T(8,128)(2,1)} %lead_hbm.1, ...), custom_call_target="tpu_custom_call" | custom-call | tf_op jit(solution)/shard_map/pallas_call | solution.py:438
  60.3 2.1 %copy.13 = f32[6,32,1024]{2,1,0:T(8,128)} copy(f32[6,32,1024]{2,1,0:T(8,128)} %get-tuple-element.18) | data formatting | bytes 1572864
  62.4 1.5 %copy.14 = f32[6,128,32]{1,2,0:T(8,128)} copy(f32[6,128,32]{1,2,0:T(8,128)} %bitcast.8) | data formatting | bytes 196608
where the time goes:
time: 64.3 us; the launch traced here: 64 us
  Pallas kernels  59.7 us (93%)
  local copies, waits for them, and re-layouts  3.63 us (6%)
  between operations  0.65 us (1%)
    pallas_call x1, Pallas kernels, body(): pl.pallas_call(functools.partial(kernel, owners, columns, slots), out_sha...  54.5 us
    pallas_call x1, Pallas kernels, body(): pl.pallas_call(functools.partial(pack_kernel, owners, columns, slots), ou...  5.22 us
    unnamed x2, local copies, waits for them, and re-layouts  3.63 us

commit v1 on v0

v1 whole, which is shorter than its diff:
```python
import functools

import jax
import jax.numpy as jnp
from jax import lax
from jax.experimental import pallas as pl
from jax.experimental.pallas import tpu as pltpu
from jax.sharding import PartitionSpec as P

DMIN = 6
STEPS = 6
TIMES = STEPS + 1
BULK = 4
INNER = 2
WINDOW = TIMES
VMEM_BYTES = 40 * 1024 * 1024

exciting_amplitude = 3.25
suppressive_amplitude = 22.0
exciting_inverse_lag = 0.1
suppressive_inverse_lag = 0.05
link_factor = 135.0
maximal_spike_frequency = 0.005
thresh = 6.0
fire_slope = 0.56
global_scaling_factor = 0.5
dt_step = 0.5

COUPLED_RATE = exciting_amplitude * exciting_inverse_lag * global_scaling_factor
NEXT_GAIN = 0.5 * dt_step * COUPLED_RATE
POTENTIAL_GAIN = (
    0.5
    * dt_step
    * (2.0 * NEXT_GAIN + dt_step * (COUPLED_RATE - 2.0 * exciting_inverse_lag * NEXT_GAIN))
)

MESH = pl.DeviceIdType.MESH


def sigmoid_spike_density(level):
    return 1.0 / (1.0 + jnp.exp(fire_slope * (thresh - level)))


def derivative(y, noise, coupled):
    curvature = (
        exciting_amplitude
        * exciting_inverse_lag
        * maximal_spike_frequency
        * sigmoid_spike_density(y[1] - y[2])
        - 2.0 * exciting_inverse_lag * y[3]
        - exciting_inverse_lag * exciting_inverse_lag * y[0]
    )
    drive = noise + 0.8 * link_factor * maximal_spike_frequency * sigmoid_spike_density(
        link_factor * y[0]
    )
    if coupled is not None:
        drive = drive + global_scaling_factor * coupled
    interneuron = (
        exciting_amplitude * exciting_inverse_lag * drive
        - 2.0 * exciting_inverse_lag * y[4]
        - exciting_inverse_lag * exciting_inverse_lag * y[1]
    )
    suppressive = (
        suppressive_amplitude
        * suppressive_inverse_lag
        * 0.25
        * link_factor
        * maximal_spike_frequency
        * sigmoid_spike_density(0.25 * link_factor * y[0])
        - 2.0 * suppressive_inverse_lag * y[5]
        - suppressive_inverse_lag * suppressive_inverse_lag * y[2]
    )
    return [y[3], y[4], y[5], curvature, interneuron, suppressive]


def advance(y, noise, coupled_now):
    first = derivative(y, noise, coupled_now)
    moved = [a + dt_step * b for a, b in zip(y, first)]
    second = derivative(moved, noise, None)
    return [a + 0.5 * dt_step * (b + c) for a, b, c in zip(y, first, second)]


def flip(index, mask):
    out = index
    bit = 1
    while bit <= mask:
        if mask & bit:
            out = out + bit * (1 - 2 * (lax.div(index, bit) % 2))
        bit *= 2
    return out


def kernel(
    owners,
    columns,
    slots,
    src_group,
    src_sub,
    delays,
    counts,
    initial_hbm,
    noise_hbm,
    history_hbm,
    weights_hbm,
    lead_hbm,
    final_out,
    sensors_out,
    sel_sub,
    sel_start,
    sel_tile,
    hist,
    state,
    noise,
    weights,
    placed,
    lead,
    lead_t,
    staged,
    landed,
    coupled,
    base,
    potential,
    bulk,
    bulk_in,
    bulk_z,
    bulk_all,
    full_in,
    full_z,
    local_sem,
    past_sem,
    send_sem,
    recv_sem,
    bulk_send,
    bulk_recv,
    bulk_z_send,
    bulk_z_recv,
    bulk_all_send,
    bulk_all_recv,
    full_send,
    full_recv,
    full_z_send,
    full_z_recv,
):
    me = lax.axis_index("grp")
    column = lax.axis_index("node")
    outer = owners // INNER
    layer = lax.div(me, INNER)
    inside = lax.rem(me, INNER)
    near = INNER * columns
    seat = inside * columns + column
    tiles = src_group.shape[0]
    cycle_len, replicas, block_len = history_hbm.shape
    piece_len = weights.shape[1]
    share = bulk.shape[1]

    loads = [
        pltpu.make_async_copy(initial_hbm, state, local_sem.at[0]),
        pltpu.make_async_copy(weights_hbm, weights.at[pl.ds(0, tiles)], local_sem.at[1]),
        pltpu.make_async_copy(noise_hbm, noise, local_sem.at[2]),
        pltpu.make_async_copy(lead_hbm, lead, local_sem.at[3]),
    ]
    past = [
        pltpu.make_async_copy(
            history_hbm.at[:, :, pl.ds(i * piece_len, piece_len)],
            hist.at[pl.ds(0, cycle_len), i],
            past_sem.at[i],
        )
        for i in range(block_len // piece_len)
    ]
    loads[0].start()
    for copy in past:
        copy.start()

    def partner(p, d):
        return flip(layer, p) * INNER + lax.rem(inside + d, INNER)

    pairs = [(p, d) for p in range(outer - 1, -1, -1) for d in range(INNER)]
    remote = [(p, d) for p, d in pairs if (p, d) != (0, 0)]
    seats = [(d, c) for d in range(INNER) for c in range(columns) if (d, c) != (0, 0)]

    barrier = pltpu.get_barrier_semaphore()
    for p, d in remote:
        pl.semaphore_signal(
            barrier, inc=1, device_id={"grp": partner(p, d)}, device_id_type=MESH
        )
    for d, c in seats:
        if c:
            pl.semaphore_signal(
                barrier,
                inc=1,
                device_id={"grp": partner(0, d), "node": lax.rem(column + c, columns)},
                device_id_type=MESH,
            )
    greeted = len(remote) + len([1 for d, c in seats if c])
    for copy in loads[1:]:
        copy.start()

    def choose(block, owner):
        live = counts[block]
        rank = jnp.int32(0)
        found = [jnp.int32(tiles)] * slots
        subs = [jnp.int32(0)] * slots
        starts = [jnp.int32(cycle_len - DMIN)] * slots
        for k in range(tiles):
            hit = jnp.logical_and(src_group[k, block] == owner, k < live)
            sub, start = src_sub[k, block], cycle_len - delays[k, block]
            for r in range(slots):
                take = jnp.logical_and(hit, rank == r)
                found[r] = jnp.where(take, k, found[r])
                subs[r] = jnp.where(take, sub, subs[r])
                starts[r] = jnp.where(take, start, starts[r])
            rank = rank + jnp.where(hit, 1, 0)
        return found, subs, starts

    def choose_out(dest, carry):
        _, subs, starts = choose(dest * columns + column, me)
        for r in range(slots):
            sel_sub[dest * slots + r] = subs[r]
            sel_start[dest * slots + r] = starts[r]
        return carry

    lax.fori_loop(0, owners, choose_out, 0)

    loads[0].wait()

    def first_fire(tile, carry):
        cols = pl.ds(pl.multiple_of(tile * piece_len, piece_len), piece_len)
        fire = sigmoid_spike_density(state[1, :, cols] - state[2, :, cols])
        hist[cycle_len, tile] = fire.astype(jnp.bfloat16)
        return carry

    lax.fori_loop(0, block_len // piece_len, first_fire, 0)
    for copy in past:
        copy.wait()

    def pack(place, carry):
        start, sub = sel_start[place], sel_sub[place]
        for t in range(TIMES):
            staged[t, place] = hist[start + t, sub]
        return carry

    lax.fori_loop(0, owners * slots, pack, 0)

    mine = pl.ds(me * slots, slots)

    def parcel(t, p, d):
        dest = partner(p, d)
        return pltpu.make_async_remote_copy(
            src_ref=staged.at[t, pl.ds(dest * slots, slots)],
            dst_ref=landed.at[t, mine],
            send_sem=send_sem.at[t, p * INNER + d],
            recv_sem=recv_sem.at[t, p * INNER + d],
            device_id={"grp": dest},
            device_id_type=MESH,
        )

    pl.semaphore_wait(barrier, greeted)
    for t in range(WINDOW):
        for p, d in remote:
            parcel(t, p, d).start()

    def keep(t, carry):
        landed[t, mine] = staged[t, mine]
        return carry

    lax.fori_loop(0, TIMES, keep, 0)

    def choose_in(owner, carry):
        found, _, _ = choose(me * columns + column, owner)
        for r in range(slots):
            sel_tile[owner * slots + r] = found[r]
        return carry

    lax.fori_loop(0, owners, choose_in, 0)
    weights[tiles] = jnp.zeros(weights.shape[1:], jnp.bfloat16)
    loads[1].wait()

    def place_weights(place, carry):
        rows = pl.ds(pl.multiple_of(place * piece_len, piece_len), piece_len)
        placed[rows, :] = weights[sel_tile[place]]
        return carry

    lax.fori_loop(0, owners * slots, place_weights, 0)
    loads[2].wait()
    loads[3].wait()
    lead_t[...] = lead[...].T

    group = INNER * slots
    depth = group * piece_len
    dot_cols = min(512, block_len)

    def absorb(t, p):
        for d in range(INNER):
            if (p, d) != (0, 0):
                parcel(t, p, d).wait_recv()
        zone = flip(layer, p)
        lhs = jnp.concatenate([landed[t, zone * group + i] for i in range(group)], axis=1)
        rows = pl.ds(pl.multiple_of(zone * depth, depth), depth)
        for start in range(0, block_len, dot_cols):
            cols = slice(start, start + dot_cols)
            part = jnp.dot(lhs, placed[rows, cols], preferred_element_type=jnp.float32)
            if p == 0:
                coupled[:, cols] = part
            else:
                coupled[:, cols] = coupled[:, cols] + part

    part_rows = 16

    def blocks(body):
        def step(i, carry):
            rows = pl.ds(pl.multiple_of(lax.rem(i, replicas // part_rows) * part_rows, part_rows), part_rows)
            cols = pl.ds(
                pl.multiple_of(lax.div(i, replicas // part_rows) * piece_len, piece_len), piece_len
            )
            body(rows, cols)
            return carry

        lax.fori_loop(0, (replicas // part_rows) * (block_len // piece_len), step, 0)

    def read(rows, cols):
        return [state[i, rows, cols] for i in range(6)]

    def move(t, out):
        def body(rows, cols):
            y = read(rows, cols)
            now = coupled[rows, cols]
            if t > 0:
                y[4] = y[4] + NEXT_GAIN * now
            y = advance(y, noise[rows, cols], now)
            if out is state:
                potential[rows, cols] = (y[1] - y[2]).astype(jnp.bfloat16)
            for i in range(6):
                out[i, rows, cols] = y[i]

        blocks(body)

    def signal():
        return jnp.dot(potential[...], lead_t[...], preferred_element_type=jnp.float32)

    def near_device(d, c):
        return {"grp": partner(0, d), "node": lax.rem(column + c, columns)}

    def full_copy(s, d, c):
        return pltpu.make_async_remote_copy(
            src_ref=full_in.at[s, seat],
            dst_ref=full_in.at[s, seat],
            send_sem=full_send.at[s, d * columns + c],
            recv_sem=full_recv.at[s, d * columns + c],
            device_id=near_device(d, c),
            device_id_type=MESH,
        )

    def full_z_copy(s, p):
        return pltpu.make_async_remote_copy(
            src_ref=full_z.at[s, layer],
            dst_ref=full_z.at[s, layer],
            send_sem=full_z_send.at[s, p],
            recv_sem=full_z_recv.at[s, p],
            device_id={"grp": partner(p, 0)},
            device_id_type=MESH,
        )

    def bulk_copy(d, c):
        other = lax.rem(inside + d, INNER) * columns + lax.rem(column + c, columns)
        return pltpu.make_async_remote_copy(
            src_ref=bulk.at[other],
            dst_ref=bulk_in.at[seat],
            send_sem=bulk_send.at[d * columns + c],
            recv_sem=bulk_recv.at[d * columns + c],
            device_id=near_device(d, c),
            device_id_type=MESH,
        )

    def bulk_z_copy(p):
        return pltpu.make_async_remote_copy(
            src_ref=bulk_z.at[layer],
            dst_ref=bulk_z.at[layer],
            send_sem=bulk_z_send.at[p],
            recv_sem=bulk_z_recv.at[p],
            device_id={"grp": partner(p, 0)},
            device_id_type=MESH,
        )

    def bulk_all_copy(d, c):
        return pltpu.make_async_remote_copy(
            src_ref=bulk_all.at[seat],
            dst_ref=bulk_all.at[seat],
            send_sem=bulk_all_send.at[d * columns + c],
            recv_sem=bulk_all_recv.at[d * columns + c],
            device_id=near_device(d, c),
            device_id_type=MESH,
        )

    def total(ref, count):
        out = ref[0]
        for i in range(1, count):
            out = out + ref[i]
        return out

    layers = list(range(1, outer))

    def start_full(s):
        full_in[s, seat] = signal()
        for d, c in seats:
            full_copy(s, d, c).start()

    def turn_full(s):
        for d, c in seats:
            full_copy(s, d, c).wait_recv()
        full_z[s, layer] = total(full_in.at[s], near)
        for p in layers:
            full_z_copy(s, p).start()

    def end_full(s):
        for p in layers:
            full_z_copy(s, p).wait_recv()
        row = (BULK + s) * replicas
        sensors_out[row : row + replicas, :] = total(full_z.at[s], outer)

    for t in range(BULK):
        for p in range(outer):
            absorb(t, p)
        move(t, state)
        part = signal()
        for i in range(replicas // share):
            bulk[t * (replicas // share) + i] = part[i * share : (i + 1) * share, :]
    for d, c in seats:
        bulk_copy(d, c).start()
    bulk_in[seat] = bulk[seat]

    t = BULK
    for p in range(outer):
        absorb(t, p)
    move(t, state)
    start_full(0)
    for d, c in seats:
        bulk_copy(d, c).wait_recv()
    bulk_z[layer] = total(bulk_in, near)
    for p in layers:
        bulk_z_copy(p).start()

    def ahead(rows, cols):
        y = read(rows, cols)
        y = advance(y, noise[rows, cols], None)
        base[rows, cols] = y[1] - y[2]

    blocks(ahead)

    t = BULK + 1
    for p in range(outer):
        absorb(t, p)
    potential[...] = (base[...] + POTENTIAL_GAIN * coupled[...]).astype(jnp.bfloat16)
    start_full(1)

    turn_full(0)
    for p in layers:
        bulk_z_copy(p).wait_recv()
    bulk_all[seat] = total(bulk_z, outer)
    for d, c in seats:
        bulk_all_copy(d, c).start()
    move(t, final_out)

    t = BULK + 2
    absorb(t, 0)
    turn_full(1)
    for p in range(1, outer):
        absorb(t, p)
    final_out[4] = final_out[4] + NEXT_GAIN * coupled[...]

    end_full(0)
    for d, c in seats:
        bulk_all_copy(d, c).wait_recv()
    for i in range(near):
        sensors_out[i * share : (i + 1) * share, :] = bulk_all[i]
    for t in range(TIMES):
        for p, d in remote:
            parcel(t, p, d).wait_send()
    for d, c in seats:
        bulk_copy(d, c).wait_send()
        bulk_all_copy(d, c).wait_send()
        for s in range(2):
            full_copy(s, d, c).wait_send()
    for p in layers:
        bulk_z_copy(p).wait_send()
        full_z_copy(0, p).wait_send()
    end_full(1)
    for p in layers:
        full_z_copy(1, p).wait_send()


def deliver(state, sensors, state_out, sensors_out, sem):
    copies = [
        pltpu.make_async_copy(sensors, sensors_out, sem.at[0]),
        pltpu.make_async_copy(state, state_out, sem.at[1]),
    ]
    for copy in copies:
        copy.start()
    for copy in copies:
        copy.wait()


def body(
    owners,
    columns,
    initial,
    afferent_noise_level,
    history,
    weights,
    lead_field,
    src_group,
    src_sub,
    delays,
    counts,
):
    cycle_len, replicas, block_len = history.shape
    tiles = src_group.shape[1]
    piece_len = weights.shape[2]
    sensors = lead_field.shape[0]
    slots = (tiles + owners - 1) // owners
    places = owners * slots
    outer = owners // INNER
    near = INNER * columns
    share = BULK * replicas // near
    smem = pl.BlockSpec(memory_space=pltpu.SMEM)
    vmem = pl.BlockSpec(memory_space=pltpu.VMEM)
    anywhere = pl.BlockSpec(memory_space=pl.ANY)
    dma = pltpu.SemaphoreType.DMA
    final, signal = pl.pallas_call(
        functools.partial(kernel, owners, columns, slots),
        out_shape=(
            pltpu.VMEM(initial.shape, jnp.float32),
            pltpu.VMEM((STEPS * replicas, sensors), jnp.float32),
        ),
        in_specs=[smem] * 4 + [pl.BlockSpec(memory_space=pltpu.HBM)] * 5,
        out_specs=(vmem, vmem),
        scratch_shapes=[
            pltpu.SMEM((places,), jnp.int32),
            pltpu.SMEM((places,), jnp.int32),
            pltpu.SMEM((places,), jnp.int32),
            pltpu.VMEM((cycle_len + 1, block_len // piece_len, replicas, piece_len), jnp.bfloat16),
            pltpu.VMEM(initial.shape, jnp.float32),
            pltpu.VMEM((replicas, block_len), jnp.float32),
            pltpu.VMEM((tiles + 1, piece_len, block_len), jnp.bfloat16),
            pltpu.VMEM((places * piece_len, block_len), jnp.bfloat16),
            pltpu.VMEM(lead_field.shape, jnp.bfloat16),
            pltpu.VMEM((block_len, sensors), jnp.bfloat16),
            pltpu.VMEM((TIMES, places, replicas, piece_len), jnp.bfloat16),
            pltpu.VMEM((TIMES, places, replicas, piece_len), jnp.bfloat16),
            pltpu.VMEM((replicas, block_len), jnp.float32),
            pltpu.VMEM((replicas, block_len), jnp.float32),
            pltpu.VMEM((replicas, block_len), jnp.bfloat16),
            pltpu.VMEM((near, share, sensors), jnp.float32),
            pltpu.VMEM((near, share, sensors), jnp.float32),
            pltpu.VMEM((outer, share, sensors), jnp.float32),
            pltpu.VMEM((near, share, sensors), jnp.float32),
            pltpu.VMEM((2, near, replicas, sensors), jnp.float32),
            pltpu.VMEM((2, outer, replicas, sensors), jnp.float32),
            dma((4,)),
            dma((block_len // piece_len,)),
            dma((TIMES, owners)),
            dma((TIMES, owners)),
            dma((near,)),
            dma((near,)),
            dma((outer,)),
            dma((outer,)),
            dma((near,)),
            dma((near,)),
            dma((2, near)),
            dma((2, near)),
            dma((2, outer)),
            dma((2, outer)),
        ],
        compiler_params=pltpu.CompilerParams(
            collective_id=0, has_side_effects=True, vmem_limit_bytes=VMEM_BYTES
        ),
    )(
        *(
            pltpu.with_memory_space_constraint(array, pltpu.HBM)
            for array in (
                src_group.T,
                src_sub.T,
                delays.T,
                counts,
                initial,
                afferent_noise_level,
                history,
                weights.reshape(tiles, piece_len, block_len),
                lead_field,
            )
        ),
    )
    final, signal = pl.pallas_call(
        deliver,
        out_shape=(
            jax.ShapeDtypeStruct(final.shape, jnp.float32),
            jax.ShapeDtypeStruct(signal.shape, jnp.float32),
        ),
        in_specs=[vmem, vmem],
        out_specs=(anywhere, anywhere),
        scratch_shapes=[dma((2,))],
        compiler_params=pltpu.CompilerParams(vmem_limit_bytes=8 * 1024 * 1024),
    )(
        pltpu.with_memory_space_constraint(final, pltpu.VMEM),
        pltpu.with_memory_space_constraint(signal, pltpu.VMEM),
    )
    signal = signal.reshape(STEPS, replicas, sensors)
    return final, jnp.transpose(signal, (0, 2, 1))


def solution(mesh):
    return jax.shard_map(
        functools.partial(body, mesh.shape["grp"], mesh.shape["node"]),
        mesh=mesh,
        in_specs=(
            P(None, None, ("grp", "node")),
            P(None, ("grp", "node")),
            P(None, None, ("grp", "node")),
            P(("grp", "node"), None, None, None),
            P(None, ("grp", "node")),
            P(),
            P(),
            P(),
            P(),
        ),
        out_specs=(P(None, None, ("grp", "node")), P()),
        check_vma=False,
    )
```

time: 64.3 us -> 51.9 us (0.81)
  Pallas kernels: 59.7 us -> 51 us
  local copies, waits for them, and re-layouts: 3.63 us -> 0 us
    pallas_call x1, Pallas kernels: 54.5 us -> 50.1 us  [body(): pl.pallas_call(functools.partial(kernel, owners, columns, slots), out_sha...]
    pallas_call x1, Pallas kernels: 5.22 us -> 0.93 us  [body(): pl.pallas_call(deliver, out_shape=(jax.ShapeDtypeStruct(final.shape, jnp....]
    unnamed x2 -> x0, local copies, waits for them, and re-layouts: 3.63 us -> none
where the time goes in v1:
time: 51.9 us; the launch traced here: 51.7 us
  Pallas kernels  51 us (98%)
  between operations  0.64 us (1%)
    pallas_call x1, Pallas kernels, body(): pl.pallas_call(functools.partial(kernel, owners, columns, slots), out_sha...  50.1 us

profile of v1, /device:TPU:0, one launch (start us, length us, event | category | flops | bytes accessed | tf_op | source)
XLA Modules:
  0.0 51.7 jit_solution(4849084403680221073)
XLA Ops:
  0.6 50.1 %shard_map.104 = (f32[6,32,1024]{2,1,0:T(8,128)S(1)}, f32[192,128]{1,0:T(8,128)S(1)}) custom-call(s32[24,32]{1,0:T(8,128)} %bitcast.8, s32[24,32]{1,0:T(8,128)} %bitcast.9, s32[24,32]{1,0:T(8,128)} %bitcast.10, s32[32]{0:T(128)} %counts.1, f32[6,32,1024]{2,1,0:T(8,128)} %initial_hbm.1, f32[32,1024]{1,0:T(8,128)} %noise_hbm.1, ...), custom_call_target="tpu_custom_call" | custom-call | tf_op jit(solution)/shard_map/pallas_call | solution.py:528
  50.7 0.9 %shard_map.105 = (f32[6,32,1024]{2,1,0:T(8,128)}, f32[192,128]{1,0:T(8,128)}) custom-call(f32[6,32,1024]{2,1,0:T(8,128)S(1)} %get-tuple-element.6.state, f32[192,128]{1,0:T(8,128)S(1)} %get-tuple-element.7.sensors), custom_call_target="tpu_custom_call" | custom-call | tf_op jit(solution)/shard_map/pallas_call | solution.py:592

commit v2 on v1

--- a/solution.py
+++ b/solution.py
@@ -12,7 +12,10 @@
 TIMES = STEPS + 1
 BULK = 4
 INNER = 2
-WINDOW = TIMES
+GROUPS = ((0,), (1, 2), (3,), (4,), (5,), (6,))
+AHEAD = 2
+STAGE = 2
+HOLD = 2
 VMEM_BYTES = 40 * 1024 * 1024
 
 exciting_amplitude = 3.25
@@ -94,10 +97,10 @@
     owners,
     columns,
     slots,
-    src_group,
-    src_sub,
-    delays,
-    counts,
+    group_hbm,
+    sub_hbm,
+    delays_hbm,
+    counts_hbm,
     initial_hbm,
     noise_hbm,
     history_hbm,
@@ -105,6 +108,11 @@
     lead_hbm,
     final_out,
     sensors_out,
+    src_group,
+    src_sub,
+    delays,
+    counts,
+    index_sem,
     sel_sub,
     sel_start,
     sel_tile,
@@ -153,6 +161,26 @@
     piece_len = weights.shape[1]
     share = bulk.shape[1]
 
+    def partner(p, d):
+        return flip(layer, p) * INNER + lax.rem(inside + d, INNER)
+
+    pairs = [(p, d) for p in range(outer - 1, -1, -1) for d in range(INNER)]
+    remote = [(p, d) for p, d in pairs if (p, d) != (0, 0)]
+    seats = [(d, c) for d in range(INNER) for c in range(columns) if (d, c) != (0, 0)]
+
+    barrier = pltpu.get_barrier_semaphore()
+    for p, d in remote:
+        pl.semaphore_signal(
+            barrier, inc=1, device_id={"grp": partner(p, d)}, device_id_type=MESH
+        )
+    for d, c in seats:
+        if c:
+            pl.semaphore_signal(
+                barrier,
+                inc=1,
+                device_id={"grp": partner(0, d), "node": lax.rem(column + c, columns)},
+                device_id_type=MESH,
+            )
     loads = [
         pltpu.make_async_copy(initial_hbm, state, local_sem.at[0]),
         pltpu.make_async_copy(weights_hbm, weights.at[pl.ds(0, tiles)], local_sem.at[1]),
@@ -167,30 +195,18 @@
         )
         for i in range(block_len // piece_len)
     ]
+    index = [
+        pltpu.make_async_copy(a, b, index_sem.at[i])
+        for i, (a, b) in enumerate(
+            ((group_hbm, src_group), (sub_hbm, src_sub), (delays_hbm, delays), (counts_hbm, counts))
+        )
+    ]
+    for copy in index:
+        copy.start()
     loads[0].start()
     for copy in past:
         copy.start()
 
-    def partner(p, d):
-        return flip(layer, p) * INNER + lax.rem(inside + d, INNER)
-
-    pairs = [(p, d) for p in range(outer - 1, -1, -1) for d in range(INNER)]
-    remote = [(p, d) for p, d in pairs if (p, d) != (0, 0)]
-    seats = [(d, c) for d in range(INNER) for c in range(columns) if (d, c) != (0, 0)]
-
-    barrier = pltpu.get_barrier_semaphore()
-    for p, d in remote:
-        pl.semaphore_signal(
-            barrier, inc=1, device_id={"grp": partner(p, d)}, device_id_type=MESH
-        )
-    for d, c in seats:
-        if c:
-            pl.semaphore_signal(
-                barrier,
-                inc=1,
-                device_id={"grp": partner(0, d), "node": lax.rem(column + c, columns)},
-                device_id_type=MESH,
-            )
     greeted = len(remote) + len([1 for d, c in seats if c])
     for copy in loads[1:]:
         copy.start()
@@ -219,6 +235,8 @@
             sel_start[dest * slots + r] = starts[r]
         return carry
 
+    for copy in index:
+        copy.wait()
     lax.fori_loop(0, owners, choose_out, 0)
 
     loads[0].wait()
@@ -233,37 +251,35 @@
     for copy in past:
         copy.wait()
 
-    def pack(place, carry):
-        start, sub = sel_start[place], sel_sub[place]
-        for t in range(TIMES):
-            staged[t, place] = hist[start + t, sub]
+    def pack(owner, carry):
+        for r in range(slots):
+            start, sub = sel_start[owner * slots + r], sel_sub[owner * slots + r]
+            for t in range(TIMES):
+                staged[owner, t, r] = hist[start + t, sub]
         return carry
 
-    lax.fori_loop(0, owners * slots, pack, 0)
-
-    mine = pl.ds(me * slots, slots)
-
-    def parcel(t, p, d):
+    lax.fori_loop(0, owners, pack, 0)
+
+    def parcel(g, p, d):
+        times = pl.ds(GROUPS[g][0], len(GROUPS[g]))
         dest = partner(p, d)
         return pltpu.make_async_remote_copy(
-            src_ref=staged.at[t, pl.ds(dest * slots, slots)],
-            dst_ref=landed.at[t, mine],
-            send_sem=send_sem.at[t, p * INNER + d],
-            recv_sem=recv_sem.at[t, p * INNER + d],
+            src_ref=staged.at[dest, times],
+            dst_ref=landed.at[me, times],
+            send_sem=send_sem.at[g, p * INNER + d],
+            recv_sem=recv_sem.at[g, p * INNER + d],
             device_id={"grp": dest},
             device_id_type=MESH,
         )
 
+    def issue(g):
+        for p, d in remote:
+            parcel(g, p, d).start()
+
     pl.semaphore_wait(barrier, greeted)
-    for t in range(WINDOW):
-        for p, d in remote:
-            parcel(t, p, d).start()
-
-    def keep(t, carry):
-        landed[t, mine] = staged[t, mine]
-        return carry
-
-    lax.fori_loop(0, TIMES, keep, 0)
+    for g in range(AHEAD):
+        issue(g)
+    landed[me] = staged[me]
 
     def choose_in(owner, carry):
         found, _, _ = choose(me * columns + column, owner)
@@ -289,20 +305,30 @@
     depth = group * piece_len
     dot_cols = min(512, block_len)
 
-    def absorb(t, p):
+    def absorb(g, p):
         for d in range(INNER):
             if (p, d) != (0, 0):
-                parcel(t, p, d).wait_recv()
+                parcel(g, p, d).wait_recv()
         zone = flip(layer, p)
-        lhs = jnp.concatenate([landed[t, zone * group + i] for i in range(group)], axis=1)
+        lhs = jnp.concatenate(
+            [
+                jnp.concatenate(
+                    [landed[zone * INNER + d, t, r] for d in range(INNER) for r in range(slots)],
+                    axis=1,
+                )
+                for t in GROUPS[g]
+            ],
+            axis=0,
+        )
+        out = slice(GROUPS[g][0] * replicas, (GROUPS[g][-1] + 1) * replicas)
         rows = pl.ds(pl.multiple_of(zone * depth, depth), depth)
         for start in range(0, block_len, dot_cols):
             cols = slice(start, start + dot_cols)
             part = jnp.dot(lhs, placed[rows, cols], preferred_element_type=jnp.float32)
             if p == 0:
-                coupled[:, cols] = part
+                coupled[out, cols] = part
             else:
-                coupled[:, cols] = coupled[:, cols] + part
+                coupled[out, cols] = coupled[out, cols] + part
 
     part_rows = 16
 
@@ -323,7 +349,7 @@
     def move(t, out):
         def body(rows, cols):
             y = read(rows, cols)
-            now = coupled[rows, cols]
+            now = coupled[pl.ds(pl.multiple_of(t * replicas + rows.start, part_rows), part_rows), cols]
             if t > 0:
                 y[4] = y[4] + NEXT_GAIN * now
             y = advance(y, noise[rows, cols], now)
@@ -417,27 +443,29 @@
         row = (BULK + s) * replicas
         sensors_out[row : row + replicas, :] = total(full_z.at[s], outer)
 
-    for t in range(BULK):
+    last = len(GROUPS) - 2
+    for g in range(last):
         for p in range(outer):
-            absorb(t, p)
-        move(t, state)
-        part = signal()
-        for i in range(replicas // share):
-            bulk[t * (replicas // share) + i] = part[i * share : (i + 1) * share, :]
-    for d, c in seats:
-        bulk_copy(d, c).start()
-    bulk_in[seat] = bulk[seat]
-
-    t = BULK
-    for p in range(outer):
-        absorb(t, p)
-    move(t, state)
-    start_full(0)
-    for d, c in seats:
-        bulk_copy(d, c).wait_recv()
-    bulk_z[layer] = total(bulk_in, near)
-    for p in layers:
-        bulk_z_copy(p).start()
+            absorb(g, p)
+            if p == STAGE and g + AHEAD <= last:
+                issue(g + AHEAD)
+        for t in GROUPS[g]:
+            move(t, state)
+            if t < BULK:
+                part = signal()
+                for i in range(replicas // share):
+                    bulk[t * (replicas // share) + i] = part[i * share : (i + 1) * share, :]
+            if t == BULK - 1:
+                for d, c in seats:
+                    bulk_copy(d, c).start()
+                bulk_in[seat] = bulk[seat]
+            if t == BULK:
+                start_full(0)
+                for d, c in seats:
+                    bulk_copy(d, c).wait_recv()
+                bulk_z[layer] = total(bulk_in, near)
+                for p in layers:
+                    bulk_z_copy(p).start()
 
     def ahead(rows, cols):
         y = read(rows, cols)
@@ -445,12 +473,18 @@
         base[rows, cols] = y[1] - y[2]
 
     blocks(ahead)
-
-    t = BULK + 1
+    if HOLD < 0:
+        issue(last + 1)
+
     for p in range(outer):
-        absorb(t, p)
-    potential[...] = (base[...] + POTENTIAL_GAIN * coupled[...]).astype(jnp.bfloat16)
+        absorb(last, p)
+        if p == HOLD:
+            issue(last + 1)
+    at = slice(GROUPS[last][0] * replicas, (GROUPS[last][0] + 1) * replicas)
+    potential[...] = (base[...] + POTENTIAL_GAIN * coupled[at, :]).astype(jnp.bfloat16)
     start_full(1)
+    if HOLD == outer:
+        issue(last + 1)
 
     turn_full(0)
     for p in layers:
@@ -458,23 +492,23 @@
     bulk_all[seat] = total(bulk_z, outer)
     for d, c in seats:
         bulk_all_copy(d, c).start()
-    move(t, final_out)
-
-    t = BULK + 2
-    absorb(t, 0)
+    move(STEPS - 1, final_out)
+
+    absorb(last + 1, 0)
     turn_full(1)
     for p in range(1, outer):
-        absorb(t, p)
-    final_out[4] = final_out[4] + NEXT_GAIN * coupled[...]
+        absorb(last + 1, p)
+    at = slice(STEPS * replicas, TIMES * replicas)
+    final_out[4] = final_out[4] + NEXT_GAIN * coupled[at, :]
 
     end_full(0)
     for d, c in seats:
         bulk_all_copy(d, c).wait_recv()
     for i in range(near):
         sensors_out[i * share : (i + 1) * share, :] = bulk_all[i]
-    for t in range(TIMES):
+    for g in range(len(GROUPS)):
         for p, d in remote:
-            parcel(t, p, d).wait_send()
+            parcel(g, p, d).wait_send()
     for d, c in seats:
         bulk_copy(d, c).wait_send()
         bulk_all_copy(d, c).wait_send()
@@ -531,9 +565,14 @@
             pltpu.VMEM(initial.shape, jnp.float32),
             pltpu.VMEM((STEPS * replicas, sensors), jnp.float32),
         ),
-        in_specs=[smem] * 4 + [pl.BlockSpec(memory_space=pltpu.HBM)] * 5,
+        in_specs=[pl.BlockSpec(memory_space=pltpu.HBM)] * 9,
         out_specs=(vmem, vmem),
         scratch_shapes=[
+            pltpu.SMEM((tiles, src_group.shape[0]), jnp.int32),
+            pltpu.SMEM((tiles, src_group.shape[0]), jnp.int32),
+            pltpu.SMEM((tiles, src_group.shape[0]), jnp.int32),
+            pltpu.SMEM(counts.shape, jnp.int32),
+            dma((4,)),
             pltpu.SMEM((places,), jnp.int32),
             pltpu.SMEM((places,), jnp.int32),
             pltpu.SMEM((places,), jnp.int32),
@@ -544,9 +583,9 @@
             pltpu.VMEM((places * piece_len, block_len), jnp.bfloat16),
             pltpu.VMEM(lead_field.shape, jnp.bfloat16),
             pltpu.VMEM((block_len, sensors), jnp.bfloat16),
-            pltpu.VMEM((TIMES, places, replicas, piece_len), jnp.bfloat16),
-            pltpu.VMEM((TIMES, places, replicas, piece_len), jnp.bfloat16),
-            pltpu.VMEM((replicas, block_len), jnp.float32),
+            pltpu.VMEM((owners, TIMES, slots, replicas, piece_len), jnp.bfloat16),
+            pltpu.VMEM((owners, TIMES, slots, replicas, piece_len), jnp.bfloat16),
+            pltpu.VMEM((TIMES * replicas, block_len), jnp.float32),
             pltpu.VMEM((replicas, block_len), jnp.float32),
             pltpu.VMEM((replicas, block_len), jnp.bfloat16),
             pltpu.VMEM((near, share, sensors), jnp.float32),
@@ -557,8 +596,8 @@
             pltpu.VMEM((2, outer, replicas, sensors), jnp.float32),
             dma((4,)),
             dma((block_len // piece_len,)),
-            dma((TIMES, owners)),
-            dma((TIMES, owners)),
+            dma((len(GROUPS), owners)),
+            dma((len(GROUPS), owners)),
             dma((near,)),
             dma((near,)),
             dma((outer,)),

time: 51.9 us -> 46.9 us (0.904)
  Pallas kernels: 51 us -> 46 us
    pallas_call x1, Pallas kernels: 50.1 us -> 45.1 us  [body(): pl.pallas_call(functools.partial(kernel, owners, columns, slots), out_sha...]
where the time goes in v2:
time: 46.9 us; the launch traced here: 46.7 us
  Pallas kernels  46 us (98%)
  between operations  0.64 us (1%)
    pallas_call x1, Pallas kernels, body(): pl.pallas_call(functools.partial(kernel, owners, columns, slots), out_sha...  45.1 us

profile of v2, /device:TPU:0, one launch (start us, length us, event | category | flops | bytes accessed | tf_op | source)
XLA Modules:
  0.0 46.7 jit_solution(13939298396074168197)
XLA Ops:
  0.6 45.1 %shard_map.104 = (f32[6,32,1024]{2,1,0:T(8,128)S(1)}, f32[192,128]{1,0:T(8,128)S(1)}) custom-call(s32[24,32]{1,0:T(8,128)} %bitcast.8, s32[24,32]{1,0:T(8,128)} %bitcast.9, s32[24,32]{1,0:T(8,128)} %bitcast.10, s32[32]{0:T(128)} %counts_hbm.1, f32[6,32,1024]{2,1,0:T(8,128)} %initial_hbm.1, f32[32,1024]{1,0:T(8,128)} %noise_hbm.1, ...), custom_call_target="tpu_custom_call" | custom-call | tf_op jit(solution)/shard_map/pallas_call | solution.py:562
  45.7 0.9 %shard_map.105 = (f32[6,32,1024]{2,1,0:T(8,128)}, f32[192,128]{1,0:T(8,128)}) custom-call(f32[6,32,1024]{2,1,0:T(8,128)S(1)} %get-tuple-element.6.state, f32[192,128]{1,0:T(8,128)S(1)} %get-tuple-element.7.sensors), custom_call_target="tpu_custom_call" | custom-call | tf_op jit(solution)/shard_map/pallas_call | solution.py:631

commit v3 on v2

--- a/solution.py
+++ b/solution.py
@@ -203,13 +203,10 @@
     ]
     for copy in index:
         copy.start()
-    loads[0].start()
     for copy in past:
         copy.start()
 
     greeted = len(remote) + len([1 for d, c in seats if c])
-    for copy in loads[1:]:
-        copy.start()
 
     def choose(block, owner):
         live = counts[block]
@@ -239,22 +236,15 @@
         copy.wait()
     lax.fori_loop(0, owners, choose_out, 0)
 
-    loads[0].wait()
-
-    def first_fire(tile, carry):
-        cols = pl.ds(pl.multiple_of(tile * piece_len, piece_len), piece_len)
-        fire = sigmoid_spike_density(state[1, :, cols] - state[2, :, cols])
-        hist[cycle_len, tile] = fire.astype(jnp.bfloat16)
-        return carry
-
-    lax.fori_loop(0, block_len // piece_len, first_fire, 0)
     for copy in past:
         copy.wait()
+    for copy in loads:
+        copy.start()
 
     def pack(owner, carry):
         for r in range(slots):
             start, sub = sel_start[owner * slots + r], sel_sub[owner * slots + r]
-            for t in range(TIMES):
+            for t in range(STEPS):
                 staged[owner, t, r] = hist[start + t, sub]
         return carry
 
@@ -279,6 +269,22 @@
     pl.semaphore_wait(barrier, greeted)
     for g in range(AHEAD):
         issue(g)
+    loads[0].wait()
+
+    def first_fire(tile, carry):
+        cols = pl.ds(pl.multiple_of(tile * piece_len, piece_len), piece_len)
+        fire = sigmoid_spike_density(state[1, :, cols] - state[2, :, cols])
+        hist[cycle_len, tile] = fire.astype(jnp.bfloat16)
+        return carry
+
+    lax.fori_loop(0, block_len // piece_len, first_fire, 0)
+    def pack_last(owner, carry):
+        for r in range(slots):
+            start, sub = sel_start[owner * slots + r], sel_sub[owner * slots + r]
+            staged[owner, STEPS, r] = hist[start + STEPS, sub]
+        return carry
+
+    lax.fori_loop(0, owners, pack_last, 0)
     landed[me] = staged[me]
 
     def choose_in(owner, carry):
@@ -330,7 +336,7 @@
             else:
                 coupled[out, cols] = coupled[out, cols] + part
 
-    part_rows = 16
+    part_rows = 32
 
     def blocks(body):
         def step(i, carry):
@@ -525,7 +531,9 @@
 def deliver(state, sensors, state_out, sensors_out, sem):
     copies = [
         pltpu.make_async_copy(sensors, sensors_out, sem.at[0]),
-        pltpu.make_async_copy(state, state_out, sem.at[1]),
+    ] + [
+        pltpu.make_async_copy(state.at[i], state_out.at[i], sem.at[1 + i])
+        for i in range(state.shape[0])
     ]
     for copy in copies:
         copy.start()
@@ -636,7 +644,7 @@
         ),
         in_specs=[vmem, vmem],
         out_specs=(anywhere, anywhere),
-        scratch_shapes=[dma((2,))],
+        scratch_shapes=[dma((1 + final.shape[0],))],
         compiler_params=pltpu.CompilerParams(vmem_limit_bytes=8 * 1024 * 1024),
     )(
         pltpu.with_memory_space_constraint(final, pltpu.VMEM),

time: 46.9 us -> 46.6 us (level)
  no operation moved by 1% of the time
where the time goes in v3:
time: 46.6 us; the launch traced here: 46.3 us
  Pallas kernels  45.7 us (98%)
  between operations  0.64 us (1%)
    pallas_call x1, Pallas kernels, body(): pl.pallas_call(functools.partial(kernel, owners, columns, slots), out_sha...  44.7 us
    pallas_call x1, Pallas kernels, body(): pl.pallas_call(deliver, out_shape=(jax.ShapeDtypeStruct(final.shape, jnp....  0.96 us

profile of v3, /device:TPU:0, one launch (start us, length us, event | category | flops | bytes accessed | tf_op | source)
XLA Modules:
  0.0 46.3 jit_solution(12542252406256880450)
XLA Ops:
  0.6 44.7 %shard_map.104 = (f32[6,32,1024]{2,1,0:T(8,128)S(1)}, f32[192,128]{1,0:T(8,128)S(1)}) custom-call(s32[24,32]{1,0:T(8,128)} %bitcast.8, s32[24,32]{1,0:T(8,128)} %bitcast.9, s32[24,32]{1,0:T(8,128)} %bitcast.10, s32[32]{0:T(128)} %counts_hbm.1, f32[6,32,1024]{2,1,0:T(8,128)} %initial_hbm.1, f32[32,1024]{1,0:T(8,128)} %noise_hbm.1, ...), custom_call_target="tpu_custom_call" | custom-call | tf_op jit(solution)/shard_map/pallas_call | solution.py:570
  45.3 1.0 %shard_map.105 = (f32[6,32,1024]{2,1,0:T(8,128)}, f32[192,128]{1,0:T(8,128)}) custom-call(f32[6,32,1024]{2,1,0:T(8,128)S(1)} %get-tuple-element.6.state, f32[192,128]{1,0:T(8,128)S(1)} %get-tuple-element.7.sensors), custom_call_target="tpu_custom_call" | custom-call | tf_op jit(solution)/shard_map/pallas_call | solution.py:639

commit v4 on v3

--- a/solution.py
+++ b/solution.py
@@ -493,15 +493,15 @@
         issue(last + 1)
 
     turn_full(0)
+    move(STEPS - 1, final_out)
+
+    absorb(last + 1, 0)
+    turn_full(1)
     for p in layers:
         bulk_z_copy(p).wait_recv()
     bulk_all[seat] = total(bulk_z, outer)
     for d, c in seats:
         bulk_all_copy(d, c).start()
-    move(STEPS - 1, final_out)
-
-    absorb(last + 1, 0)
-    turn_full(1)
     for p in range(1, outer):
         absorb(last + 1, p)
     at = slice(STEPS * replicas, TIMES * replicas)

time: 46.6 us -> 47.7 us (1.024)
  Pallas kernels: 45.7 us -> 46.8 us
    pallas_call x1, Pallas kernels: 44.7 us -> 45.9 us  [body(): pl.pallas_call(functools.partial(kernel, owners, columns, slots), out_sha...]
where the time goes in v4:
time: 47.7 us; the launch traced here: 47.5 us
  Pallas kernels  46.8 us (98%)
  between operations  0.64 us (1%)
    pallas_call x1, Pallas kernels, body(): pl.pallas_call(functools.partial(kernel, owners, columns, slots), out_sha...  45.9 us
    pallas_call x1, Pallas kernels, body(): pl.pallas_call(deliver, out_shape=(jax.ShapeDtypeStruct(final.shape, jnp....  0.96 us

profile of v4, /device:TPU:0, one launch (start us, length us, event | category | flops | bytes accessed | tf_op | source)
XLA Modules:
  0.0 47.5 jit_solution(5226518174177288317)
XLA Ops:
  0.6 45.9 %shard_map.104 = (f32[6,32,1024]{2,1,0:T(8,128)S(1)}, f32[192,128]{1,0:T(8,128)S(1)}) custom-call(s32[24,32]{1,0:T(8,128)} %bitcast.8, s32[24,32]{1,0:T(8,128)} %bitcast.9, s32[24,32]{1,0:T(8,128)} %bitcast.10, s32[32]{0:T(128)} %counts_hbm.1, f32[6,32,1024]{2,1,0:T(8,128)} %initial_hbm.1, f32[32,1024]{1,0:T(8,128)} %noise_hbm.1, ...), custom_call_target="tpu_custom_call" | custom-call | tf_op jit(solution)/shard_map/pallas_call | solution.py:570
  46.5 1.0 %shard_map.105 = (f32[6,32,1024]{2,1,0:T(8,128)}, f32[192,128]{1,0:T(8,128)}) custom-call(f32[6,32,1024]{2,1,0:T(8,128)S(1)} %get-tuple-element.6.state, f32[192,128]{1,0:T(8,128)S(1)} %get-tuple-element.7.sensors), custom_call_target="tpu_custom_call" | custom-call | tf_op jit(solution)/shard_map/pallas_call | solution.py:639
